TPU v7x, 32 devices: a whole 2x2x4 slice. The times are simulated.
32 devices in a mesh: dp: 8 (over y, x, core), expert: 4 (over z).
Axes of the slice: x: 2, y: 2, z: 4, core: 2. Of those that a mesh axis runs over, the one named last changes fastest.
Arguments:
- tokens: bfloat16 [4096, 2048], P(('dp', 'expert')), may hold values from -6 to 6
- out_grad: bfloat16 [4096, 2048], P(('dp', 'expert')), may hold values from -6 to 6
- gate_prob: float32 [4096, 1], P(('dp', 'expert')), may hold values from 0.2 to 1
- routing: int32 [4096, 1], P(('dp', 'expert')), may hold values from 0 to 3; in each aligned block of 128 rows (0 to 127, 128 to 255, ...) at most 64 rows name the same one
- expert_weights: bfloat16 [4, 2048, 1152], P('expert'), may hold values from -0.125 to 0.125
Outputs:
- input_grad: bfloat16 [4096, 2048], P(('dp', 'expert'))
- weight_grad: float32 [4, 2048, 1152], P('expert', 'dp')
Inputs may be any that keep to these rules, and one draw needn't show every extreme that they name: `routing`: among the tokens of one device at most 64 go to any one expert; in some devices' tokens an expert gets exactly 64.
All inputs are finite; a program needn't handle non-finite values.
Results may differ from a plain program's by a relative error of at most 0.014.
Values may be sent and summed in bfloat16 or wider, within the bound.
A program may use at most 64 MiB of HBM per device.

v0:
```python
import jax
import jax.numpy as jnp
from jax import lax
from jax.sharding import PartitionSpec as P


def slot_of(route_block, capacity, experts):
    onehot = (route_block[:, None] == jnp.arange(experts, dtype=jnp.int32)[None, :]).astype(
        jnp.int32
    )
    before = jnp.cumsum(onehot, axis=0) - onehot
    position = jnp.sum(before * onehot, axis=1)
    return route_block * capacity + position


def expert_rows(weights, rows_in, grad_in):
    hidden_width = weights.shape[1] // 3
    pair_weights = weights[:, : 2 * hidden_width]
    down_weights = weights[:, 2 * hidden_width :]
    pre_act = jnp.dot(rows_in, pair_weights, preferred_element_type=jnp.float32)
    pre_gate = pre_act[:, :hidden_width]
    pre_up = pre_act[:, hidden_width:]
    sigmoid_gate = jax.nn.sigmoid(pre_gate)
    active = pre_gate * sigmoid_gate
    hidden = (active * pre_up).astype(jnp.bfloat16)
    grad_hidden = jnp.dot(grad_in, down_weights, preferred_element_type=jnp.float32)
    grad_gate = grad_hidden * pre_up * (sigmoid_gate * (1.0 + pre_gate * (1.0 - sigmoid_gate)))
    grad_up = grad_hidden * active
    grad_pair = jnp.concatenate(
        [grad_gate.astype(jnp.bfloat16), grad_up.astype(jnp.bfloat16)], axis=1
    )
    returned = lax.dot_general(
        grad_pair, pair_weights, (((1,), (1,)), ((), ())), preferred_element_type=jnp.float32
    )
    return (returned.astype(jnp.bfloat16), hidden, grad_pair)


def weight_term(rows_in, grad_in, hidden, grad_pair, grad_scale):
    contract = (((0,), (0,)), ((), ()))
    first_part = lax.dot_general(rows_in, grad_pair, contract, preferred_element_type=jnp.float32)
    second = lax.dot_general(grad_in, hidden, contract, preferred_element_type=jnp.float32)
    return grad_scale * jnp.concatenate([first_part, second], axis=1)


def sum_weights(rows_in, grad_in, hidden, grad_pair, grad_scale):
    return lax.psum_scatter(
        weight_term(rows_in, grad_in, hidden, grad_pair, grad_scale).astype(jnp.bfloat16),
        "dp",
        scatter_dimension=0,
        tiled=True,
    ).astype(jnp.float32)


def send_back(returned):
    return lax.all_to_all(returned, "expert", split_axis=0, concat_axis=0, tiled=True)


def local(tokens, out_grad, gate_prob, routing, expert_weights):
    tok_dev, model_width = tokens.shape
    experts = lax.axis_size("expert")
    replicas = lax.axis_size("dp")
    capacity = 2 * tok_dev // experts
    share_rows = model_width // replicas
    grad_scale = float(tok_dev * replicas) ** (-0.5)
    weights = expert_weights[0]
    hidden_width = weights.shape[1] // 3
    scaled = (gate_prob * out_grad.astype(jnp.float32)).astype(jnp.bfloat16)
    slot_index = slot_of(routing[:, 0], capacity, experts)
    dispatch_table = (
        jnp.arange(experts * capacity, dtype=jnp.int32)[:, None] == slot_index[None, :]
    ).astype(jnp.bfloat16)
    send_x = (
        jnp.dot(dispatch_table, tokens, preferred_element_type=jnp.float32)
        .astype(jnp.bfloat16)
        .reshape(experts, capacity, model_width)
    )
    send_g = (
        jnp.dot(dispatch_table, scaled, preferred_element_type=jnp.float32)
        .astype(jnp.bfloat16)
        .reshape(experts, capacity, model_width)
    )
    recv_x, recv_g = (
        lax.all_to_all(send_x, "expert", split_axis=0, concat_axis=0, tiled=True),
        lax.all_to_all(send_g, "expert", split_axis=0, concat_axis=0, tiled=True),
    )
    rows_in = recv_x.reshape(experts * capacity, model_width)
    grad_in = recv_g.reshape(experts * capacity, model_width)
    returned, hidden, grad_pair = expert_rows(weights, rows_in, grad_in)
    returned = returned.reshape(experts, capacity, model_width)
    arrived = send_back(returned)
    summed = sum_weights(rows_in, grad_in, hidden, grad_pair, grad_scale)
    input_grad = lax.dot_general(
        dispatch_table,
        arrived.reshape(experts * capacity, model_width),
        (((0,), (0,)), ((), ())),
        preferred_element_type=jnp.float32,
    ).astype(jnp.bfloat16)
    return (input_grad, summed.reshape(1, share_rows, 3 * hidden_width))


def solution(mesh):
    in_specs = (
        P(("dp", "expert"), None),
        P(("dp", "expert"), None),
        P(("dp", "expert"), None),
        P(("dp", "expert"), None),
        P("expert", None, None),
    )
    out_specs = (P(("dp", "expert"), None), P("expert", "dp", None))
    return jax.shard_map(local, mesh=mesh, in_specs=in_specs, out_specs=out_specs, check_vma=False)
```

profile of v0, /device:TPU:0, one launch (start us, length us, event | category | flops | bytes accessed | tf_op | source)
XLA Modules:
  0.0 147.1 jit_solution(2078213292163461585)
XLA Ops:
  7.2 0.8 fusion.17
  8.0 0.2 reduce_window_sum.11
  8.2 0.8 select_reduce_fusion
  9.0 0.7 multiply_add_fusion
  9.7 1.4 convolution_convert_fusion
  11.1 6.3 %all-to-all-start.1 = ((bf16[4,64,2048]{2,1,0:T(8,128)(2,1)}), bf16[4,64,2048]{2,1,0:T(8,128)(2,1)S(1)}, u32[]{:S(2)}, u32[]{:S(2)}) async-start(bf16[4,64,2048]{2,1,0:T(8,128)(2,1)} %bitcast.5), calls=%async_computation.1 | async-start | bytes 2097152 | tf_op jit(solution)/shard_map/all_to_all | solution.py:83
  17.4 2.5 %convolution_convert_fusion.1 = bf16[256,2048]{1,0:T(8,128)(2,1)} fusion(bf16[128,2048]{1,0:T(8,128)(2,1)} %param.6, f32[128]{0:T(128)} %bitcast.27, s32[128]{0:T(128)S(1)} %multiply_add_fusion), kind=kOutput, calls=%fused_computation.7 | convolution fusion | flops 135561216 | bytes 1573888 | tf_op jit(solution)/shard_map/dot_general | solution.py:78
  19.9 23.2 %all-to-all-done.1 = bf16[4,64,2048]{2,1,0:T(8,128)(2,1)S(1)} async-done(((bf16[4,64,2048]{2,1,0:T(8,128)(2,1)}), bf16[4,64,2048]{2,1,0:T(8,128)(2,1)S(1)}, u32[]{:S(2)}, u32[]{:S(2)}) %all-to-all-start.1) | async-done | bytes 1048608 | tf_op jit(solution)/shard_map/all_to_all | solution.py:83
  43.1 3.5 %all-to-all-start = ((bf16[4,64,2048]{2,1,0:T(8,128)(2,1)}), bf16[4,64,2048]{2,1,0:T(8,128)(2,1)S(1)}, u32[]{:S(2)}, u32[]{:S(2)}) async-start(bf16[4,64,2048]{2,1,0:T(8,128)(2,1)} %bitcast.2), calls=%async_computation | async-start | bytes 2097152 | tf_op jit(solution)/shard_map/all_to_all | solution.py:84
  46.7 2.9 %fusion.3 = f32[256,768]{1,0:T(8,128)S(1)} fusion(bf16[256,2048]{1,0:T(8,128)(2,1)S(1)} %bitcast.19, bf16[2048,1152]{1,0:T(8,128)(2,1)} %bitcast.28), kind=kOutput, calls=%fused_computation.4 | convolution fusion | flops 805306368 | bytes 4980736 | tf_op jit(solution)/shard_map/dot_general | solution.py:20
  49.6 22.3 %all-to-all-done = bf16[4,64,2048]{2,1,0:T(8,128)(2,1)S(1)} async-done(((bf16[4,64,2048]{2,1,0:T(8,128)(2,1)}), bf16[4,64,2048]{2,1,0:T(8,128)(2,1)S(1)}, u32[]{:S(2)}, u32[]{:S(2)}) %all-to-all-start) | async-done | bytes 1048608 | tf_op jit(solution)/shard_map/all_to_all | solution.py:84
  71.9 2.2 %multiply_convert_fusion.4 = (bf16[256,384]{1,0:T(8,128)(2,1)S(1)}, bf16[256,384]{1,0:T(8,128)(2,1)S(1)}) fusion(f32[256,768]{1,0:T(8,128)S(1)} %fusion.3, bf16[256,2048]{1,0:T(8,128)(2,1)S(1)} %bitcast.22, bf16[2048,1152]{1,0:T(8,128)(2,1)} %bitcast.29), kind=kOutput, calls=%fused_computation.18 | convolution fusion | flops 403931136 | bytes 3801088 | tf_op jit(solution)/shard_map/dot_general | solution.py:26
  74.1 0.6 fusion.13
  74.8 0.1 copy-done.3
  74.8 3.7 %fusion.12 = f32[2048,768]{0,1:T(8,128)} fusion(bf16[256,2048]{1,0:T(8,128)(2,1)S(1)} %bitcast.20, bf16[256,384]{1,0:T(8,128)(2,1)S(1)} %get-tuple-element.5, bf16[256,384]{1,0:T(8,128)(2,1)S(1)} %get-tuple-element.4), kind=kOutput, calls=%fused_computation.21 | convolution fusion | flops 806092800 | bytes 7733248 | tf_op jit(solution)/shard_map/dot_general | solution.py:40
  78.5 6.2 %fusion = bf16[2048,1152]{0,1:T(8,128)(2,1)} fusion(f32[2048,384]{0,1:T(8,128)S(1)} %fusion.13, f32[2048,768]{0,1:T(8,128)} %fusion.12), kind=kLoop, calls=%fused_computation.1 | loop fusion | flops 7077888 | bytes 14155776 | tf_op jit(solution)/shard_map/convert_element_type | solution.py:47
  84.8 0.9 copy-done.2
  85.7 0.1 copy-done.4
  85.8 2.9 %fusion.5 = bf16[256,2048]{1,0:T(8,128)(2,1)S(1)} fusion(bf16[2048,1152]{1,0:T(8,128)(2,1)} %bitcast.30, bf16[256,384]{1,0:T(8,128)(2,1)S(1)} %copy-done.4, bf16[256,384]{1,0:T(8,128)(2,1)S(1)} %copy-done.2), kind=kOutput, calls=%fused_computation.8 | convolution fusion | flops 806617088 | bytes 4587520 | tf_op jit(solution)/shard_map/dot_general | solution.py:32
  88.7 27.7 %all_to_all.15 = bf16[4,64,2048]{2,1,0:T(8,128)(2,1)S(1)} all-to-all(bf16[4,64,2048]{2,1,0:T(8,128)(2,1)S(1)} %bitcast.24), channel_id=1, replica_groups=mesh['dp'=8,'expert'=4] {'expert'}, dimensions={0} | all-to-all | bytes 2097152 | tf_op jit(solution)/shard_map/all_to_all | solution.py:55
  116.4 1.1 convolution_convert_fusion.2
  117.6 20.2 %reduce-scatter.2.cloned.1.call-done = bf16[256,1152]{0,1:T(8,128)(2,1)} async-done(((bf16[2048,1152]{0,1:T(8,128)(2,1)}), bf16[256,1152]{0,1:T(8,128)(2,1)}) %reduce-scatter.2.cloned.1.call-update) | async-done | bytes 589840 | tf_op jit(solution)/shard_map/reduce_scatter | solution.py:46
  137.8 1.1 bitcast_convert_fusion
  138.9 1.4 copy.7
  (9 shorter events, 0.1 us)
Async XLA Ops:
  7.2 2.5 %copy-start = (bf16[128,2048]{1,0:T(8,128)(2,1)S(1)}, bf16[128,2048]{1,0:T(8,128)(2,1)}, u32[]{:S(2)}) copy-start(bf16[128,2048]{1,0:T(8,128)(2,1)} %param.5) | copy-start | bytes 1572868
  11.1 32.1 %all-to-all-start.1 = ((bf16[4,64,2048]{2,1,0:T(8,128)(2,1)}), bf16[4,64,2048]{2,1,0:T(8,128)(2,1)S(1)}, u32[]{:S(2)}, u32[]{:S(2)}) async-start(bf16[4,64,2048]{2,1,0:T(8,128)(2,1)} %bitcast.5), calls=%async_computation.1 | async-start | bytes 2097152 | tf_op jit(solution)/shard_map/all_to_all | solution.py:83
  43.1 28.8 %all-to-all-start = ((bf16[4,64,2048]{2,1,0:T(8,128)(2,1)}), bf16[4,64,2048]{2,1,0:T(8,128)(2,1)S(1)}, u32[]{:S(2)}, u32[]{:S(2)}) async-start(bf16[4,64,2048]{2,1,0:T(8,128)(2,1)} %bitcast.2), calls=%async_computation | async-start | bytes 2097152 | tf_op jit(solution)/shard_map/all_to_all | solution.py:84
  46.6 91.1 %reduce-scatter.2.cloned.1.call-start = ((), (), s32[]{:S(2)}) async-start(), calls=%async_computation.4 | async-start | bytes 5308416 | tf_op jit(solution)/shard_map/reduce_scatter | solution.py:46
  74.1 0.7 copy-start.1
  74.1 0.7 copy-start.3
  84.8 0.9 copy-start.2
  84.8 1.0 copy-start.4
Sparse Core Ops, SparseCore 0:
  84.9 52.7 reduce-scatter.1
where the time goes:
time: 148 us; the launch traced here: 147 us
  waiting for transfers between devices  65.7 us (44%)
  blocking collectives  27.7 us (19%)
  matrix products  17.4 us (12%)
  between operations  14.1 us (10%)
  starting transfers between devices  9.9 us (7%)
  other arithmetic  9.85 us (7%)
  local copies, waits for them, and re-layouts  2.47 us (2%)
    all_to_all x1, blocking collectives, send_back(): lax.all_to_all(returned, 'expert', split_axis=0, concat_axis=0, tiled=True)  27.7 us
    all_to_all x1, waiting for transfers between devices, local(): lax.all_to_all(send_x, 'expert', split_axis=0, concat_axis=0, tiled=True)  23.2 us
    all_to_all x1, waiting for transfers between devices, local(): lax.all_to_all(send_g, 'expert', split_axis=0, concat_axis=0, tiled=True)  22.3 us
    reduce_scatter x1, waiting for transfers between devices, sum_weights(): lax.psum_scatter(weight_term(rows_in, grad_in, hidden, grad_pair, grad_sc...  20.2 us
    all_to_all x1, starting transfers between devices, local(): lax.all_to_all(send_x, 'expert', split_axis=0, concat_axis=0, tiled=True)  6.35 us
    convert_element_type x1, other arithmetic, sum_weights(): weight_term(rows_in, grad_in, hidden, grad_pair, grad_scale)  6.25 us
    dot_general x1, matrix products, weight_term(): lax.dot_general(rows_in, grad_pair, contract, preferred_element_type=jnp....  3.69 us
    all_to_all x1, starting transfers between devices, local(): lax.all_to_all(send_g, 'expert', split_axis=0, concat_axis=0, tiled=True)  3.52 us
  transfers between devices with their start and end apart: 3, of which 3 were waited for; matrix products, arithmetic and copies ran while one was open for 6% of the time, Pallas kernels for 0%

commit v1 on v0

v1 whole, which is shorter than its diff:
```python
import functools
import math
import jax
import jax.numpy as jnp
from jax import lax
from jax.experimental import pallas as pl
from jax.experimental.pallas import tpu as pltpu
from jax.sharding import PartitionSpec as P

MESH = pl.DeviceIdType.MESH
F32 = jnp.float32
BF16 = jnp.bfloat16


def xor(value, step):
    total, bit = 0, 1
    result = value
    while bit <= step:
        if step & bit:
            result = result + bit - 2 * bit * (lax.rem(lax.div(value, bit), 2))
        bit *= 2
    return result


def plan(n_expert, n_dp):
    half = n_expert // 2
    near = list(range(1, half))
    far = list(range(n_expert - 1, half - 1, -1))
    chips = n_dp // 2
    side = math.isqrt(chips)
    while chips % side:
        side -= 1
    return near, far, chips // side, side


def body(
    n_expert,
    n_dp,
    cap,
    tokens_ref,
    out_grad_ref,
    gate_ref,
    route_col_ref,
    route_row_ref,
    w_hbm,
    in_grad_ref,
    w_grad_ref,
    w_ref,
    send_x,
    send_g,
    recv_x,
    recv_g,
    ret,
    arrived,
    pair,
    hidden,
    part,
    recv_a,
    send_b,
    recv_b,
    send_c,
    recv_c,
    w_sem,
    dx_s,
    dx_r,
    dg_s,
    dg_r,
    rt_s,
    rt_r,
    a_s,
    a_r,
    b_s,
    b_r,
    c_s,
    c_r,
):
    near, far, na, nb = plan(n_expert, n_dp)
    me = lax.axis_index("expert")
    dp = lax.axis_index("dp")
    tok, width = tokens_ref.shape
    hid = w_ref.shape[1] // 3
    slots = n_expert * cap
    half_rows = slots // 2
    share = width // n_dp
    grad_scale = float(tok * n_dp) ** (-0.5)
    core = lax.rem(dp, 2)
    chip = lax.div(dp, 2)
    pos_hi, pos_lo = lax.div(chip, na), lax.rem(chip, na)
    if na == nb:
        a = jnp.where(core == 0, pos_lo, pos_hi)
        b = jnp.where(core == 0, pos_hi, pos_lo)
    else:
        a, b = pos_lo, pos_hi

    def chip_of(a_at, b_at):
        plain = b_at * na + a_at
        if na == nb:
            return jnp.where(core == 0, plain, a_at * na + b_at)
        return plain

    def dp_of(a_at, b_at):
        return chip_of(a_at, b_at) * 2 + core

    w_copy = pltpu.make_async_copy(w_hbm.at[0], w_ref, w_sem)
    w_copy.start()

    barrier = pltpu.get_barrier_semaphore()
    partner = dp + 1 - 2 * core
    greeted = 0
    for k in near + far:
        pl.semaphore_signal(barrier, inc=1, device_id={"expert": xor(me, k)}, device_id_type=MESH)
        greeted += 1
    pl.semaphore_signal(barrier, inc=1, device_id={"dp": partner}, device_id_type=MESH)
    greeted += 1
    for s in range(1, na):
        pl.semaphore_signal(
            barrier, inc=1, device_id={"dp": dp_of(lax.rem(a + s, na), b)}, device_id_type=MESH
        )
        greeted += 1
    for t in range(1, nb):
        pl.semaphore_signal(
            barrier, inc=1, device_id={"dp": dp_of(a, lax.rem(b + t, nb))}, device_id_type=MESH
        )
        greeted += 1

    route_row = route_row_ref[...]
    route_col = route_col_ref[...]
    row_i = lax.broadcasted_iota(jnp.int32, (tok, tok), 0)
    col_i = lax.broadcasted_iota(jnp.int32, (tok, tok), 1)
    same = route_col == route_row
    pos_row = jnp.sum(jnp.where(same & (row_i < col_i), 1.0, 0.0), axis=0, keepdims=True)
    pos_col = jnp.sum(jnp.where(same & (col_i < row_i), 1.0, 0.0), axis=1, keepdims=True)
    slot_row = route_row.astype(F32) * cap + pos_row
    slot_col = route_col.astype(F32) * cap + pos_col
    slot_at = lax.broadcasted_iota(jnp.int32, (slots, tok), 0).astype(F32)
    table = jnp.where(slot_at == slot_row, 1.0, 0.0).astype(BF16)
    slot_of = lax.broadcasted_iota(jnp.int32, (tok, slots), 1).astype(F32)
    table_t = jnp.where(slot_of == slot_col, 1.0, 0.0).astype(BF16)

    send_x[...] = jnp.dot(table, tokens_ref[...], preferred_element_type=F32).astype(BF16)
    scaled = (gate_ref[...] * out_grad_ref[...].astype(F32)).astype(BF16)
    send_g[...] = jnp.dot(table, scaled, preferred_element_type=F32).astype(BF16)

    def rows_of(index):
        return pl.ds(pl.multiple_of(index * cap, cap), cap)

    pl.semaphore_wait(barrier, greeted)

    def dispatch(k, src, dst, s_sem, r_sem):
        peer = xor(me, k)
        return pltpu.make_async_remote_copy(
            src_ref=src.at[rows_of(peer)],
            dst_ref=dst.at[rows_of(me)],
            send_sem=s_sem.at[k],
            recv_sem=r_sem.at[k],
            device_id={"expert": peer},
            device_id_type=MESH,
        )

    x_copies = {k: dispatch(k, send_x, recv_x, dx_s, dx_r) for k in near + far}
    g_copies = {k: dispatch(k, send_g, recv_g, dg_s, dg_r) for k in near + far}
    returns = {k: dispatch(k, ret, arrived, rt_s, rt_r) for k in near + far}
    for k in near + far:
        x_copies[k].start()
        g_copies[k].start()

    recv_x[rows_of(me)] = send_x[rows_of(me)]
    recv_g[rows_of(me)] = send_g[rows_of(me)]
    w_copy.wait()

    mine = lax.div(me, n_expert // 2) if n_expert > 1 else 0

    def forward(start):
        rows = pl.ds(pl.multiple_of(start, cap), half_rows)
        x = recv_x[rows]
        pre_gate = jnp.dot(x, w_ref[:, :hid], preferred_element_type=F32)
        pre_up = jnp.dot(x, w_ref[:, hid : 2 * hid], preferred_element_type=F32)
        grad_hidden = jnp.dot(recv_g[rows], w_ref[:, 2 * hid :], preferred_element_type=F32)
        sig = jax.nn.sigmoid(pre_gate)
        active = pre_gate * sig
        hidden[rows] = (active * pre_up).astype(BF16)
        grad_gate = grad_hidden * pre_up * (sig * (1.0 + pre_gate * (1.0 - sig)))
        pair[rows, :hid] = grad_gate.astype(BF16)
        pair[rows, hid:] = (grad_hidden * active).astype(BF16)

    def backward(start):
        rows = pl.ds(pl.multiple_of(start, cap), half_rows)
        tile = min(512, width)

        @pl.loop(0, width // tile)
        def _(j):
            at = pl.ds(pl.multiple_of(j * tile, tile), tile)
            ret[rows, at] = lax.dot_general(
                pair[rows],
                w_ref[at, : 2 * hid],
                (((1,), (1,)), ((), ())),
                preferred_element_type=F32,
            ).astype(BF16)

    first_half = mine * half_rows
    other_half = (1 - mine) * half_rows
    for k in near:
        x_copies[k].wait_recv()
        g_copies[k].wait_recv()
    forward(first_half)
    backward(first_half)
    for k in near:
        returns[k].start()
    arrived[rows_of(me)] = ret[rows_of(me)]
    for k in far:
        x_copies[k].wait_recv()
        g_copies[k].wait_recv()
    forward(other_half)
    backward(other_half)
    for k in far:
        returns[k].start()

    def weight_rows(start, size):
        at = pl.ds(pl.multiple_of(start, size), size)
        contract = (((0,), (0,)), ((), ()))
        part[at, : 2 * hid] = (
            grad_scale
            * lax.dot_general(recv_x[:, at], pair[...], contract, preferred_element_type=F32)
        ).astype(BF16)
        part[at, 2 * hid :] = (
            grad_scale
            * lax.dot_general(recv_g[:, at], hidden[...], contract, preferred_element_type=F32)
        ).astype(BF16)

    def band(chip_at, core_at):
        return pl.ds(pl.multiple_of((chip_at * 2 + core_at) * share, share), share)

    items = [(s, t) for s in range(1, na) for t in list(range(1, nb)) + [0]]
    items += [(0, t) for t in list(range(1, nb)) + [0]]

    def item_chip(s, t):
        return chip_of(lax.rem(a + s, na), lax.rem(b + t, nb))

    banded = share % 128 == 0
    if not banded:

        @pl.loop(0, width // 256)
        def _(j):
            weight_rows(j * 256, 256)

    def pair_copy(index, chip_at):
        rows = band(chip_at, 1 - core)
        return pltpu.make_async_remote_copy(
            src_ref=part.at[rows],
            dst_ref=recv_a.at[pl.ds(pl.multiple_of(chip_at * share, share), share)],
            send_sem=a_s.at[index],
            recv_sem=a_r.at[index],
            device_id={"dp": partner},
            device_id_type=MESH,
        )

    def partner_chip(s, t):
        if na == nb:
            a_at, b_at = lax.rem(b + s, na), lax.rem(a + t, nb)
            return jnp.where(core == 1, b_at * na + a_at, a_at * na + b_at)
        return item_chip(s, t)

    a_copies = []
    for index, (s, t) in enumerate(items):
        chip_at = partner_chip(s, t)
        if banded:
            weight_rows((chip_at * 2 + 1 - core) * share, share)
        copy = pair_copy(index, chip_at)
        copy.start()
        a_copies.append(copy)

    def pair_sum(index, s, t):
        chip_at = item_chip(s, t)
        a_copies[index].wait_recv()
        return (
            part[band(chip_at, core)].astype(F32)
            + recv_a[pl.ds(pl.multiple_of(chip_at * share, share), share)].astype(F32)
        )

    if banded:
        for s, t in items:
            weight_rows((item_chip(s, t) * 2 + core) * share, share)

    b_copies = {}
    for index, (s, t) in enumerate(items):
        if s == 0:
            continue
        at = (s - 1) * nb + t
        send_b[at] = pair_sum(index, s, t).astype(BF16)
        copy = pltpu.make_async_remote_copy(
            src_ref=send_b.at[at],
            dst_ref=recv_b.at[at],
            send_sem=b_s.at[at],
            recv_sem=b_r.at[at],
            device_id={"dp": dp_of(lax.rem(a + s, na), b)},
            device_id_type=MESH,
        )
        copy.start()
        b_copies[s, t] = copy
    c_copies = {}
    for index, (s, t) in enumerate(items):
        if s > 0:
            continue
        total = pair_sum(index, s, t)
        for s_from in range(1, na):
            b_copies[s_from, t].wait_recv()
            total = total + recv_b[(s_from - 1) * nb + t].astype(F32)
        if t > 0:
            send_c[t - 1] = total.astype(BF16)
            copy = pltpu.make_async_remote_copy(
                src_ref=send_c.at[t - 1],
                dst_ref=recv_c.at[t - 1],
                send_sem=c_s.at[t - 1],
                recv_sem=c_r.at[t - 1],
                device_id={"dp": dp_of(a, lax.rem(b + t, nb))},
                device_id_type=MESH,
            )
            copy.start()
            c_copies[t] = copy
        else:
            w_grad_ref[0] = total
    for t in range(1, nb):
        c_copies[t].wait_recv()
        w_grad_ref[0] += recv_c[t - 1].astype(F32)

    for k in near + far:
        returns[k].wait_recv()
    in_grad_ref[...] = jnp.dot(table_t, arrived[...], preferred_element_type=F32).astype(BF16)

    for k in near + far:
        x_copies[k].wait_send()
        g_copies[k].wait_send()
        returns[k].wait_send()
    for copy in a_copies + list(b_copies.values()) + list(c_copies.values()):
        copy.wait_send()


def local(n_expert, n_dp, tokens, out_grad, gate_prob, routing, expert_weights):
    tok, width = tokens.shape
    full = expert_weights.shape[2]
    hid = full // 3
    cap = max(16, 2 * tok // n_expert)
    slots = n_expert * cap
    share = width // n_dp
    _, _, na, nb = plan(n_expert, n_dp)
    chips = na * nb
    n_b, n_c = max(1, (na - 1) * nb), max(1, nb - 1)
    dma = pltpu.SemaphoreType.DMA
    vmem = pl.BlockSpec(memory_space=pltpu.VMEM)
    return pl.pallas_call(
        functools.partial(body, n_expert, n_dp, cap),
        out_shape=(
            jax.ShapeDtypeStruct((tok, width), BF16),
            jax.ShapeDtypeStruct((1, share, full), F32),
        ),
        in_specs=[vmem] * 5 + [pl.BlockSpec(memory_space=pl.ANY)],
        out_specs=(vmem, vmem),
        scratch_shapes=[
            pltpu.VMEM((width, full), BF16),
            pltpu.VMEM((slots, width), BF16),
            pltpu.VMEM((slots, width), BF16),
            pltpu.VMEM((slots, width), BF16),
            pltpu.VMEM((slots, width), BF16),
            pltpu.VMEM((slots, width), BF16),
            pltpu.VMEM((slots, width), BF16),
            pltpu.VMEM((slots, 2 * hid), BF16),
            pltpu.VMEM((slots, hid), BF16),
            pltpu.VMEM((width, full), BF16),
            pltpu.VMEM((chips * share, full), BF16),
            pltpu.VMEM((n_b, share, full), BF16),
            pltpu.VMEM((n_b, share, full), BF16),
            pltpu.VMEM((n_c, share, full), BF16),
            pltpu.VMEM((n_c, share, full), BF16),
            dma,
            dma((n_expert,)),
            dma((n_expert,)),
            dma((n_expert,)),
            dma((n_expert,)),
            dma((n_expert,)),
            dma((n_expert,)),
            dma((chips,)),
            dma((chips,)),
            dma((n_b,)),
            dma((n_b,)),
            dma((n_c,)),
            dma((n_c,)),
        ],
        compiler_params=pltpu.CompilerParams(
            collective_id=0, has_side_effects=True, vmem_limit_bytes=60 * 1024 * 1024
        ),
        name="moe_backward",
    )(tokens, out_grad, gate_prob, routing, routing.reshape(1, tok), expert_weights)


def solution(mesh):
    tokens_spec = P(("dp", "expert"), None)
    return jax.shard_map(
        functools.partial(local, mesh.shape["expert"], mesh.shape["dp"]),
        mesh=mesh,
        in_specs=(tokens_spec, tokens_spec, tokens_spec, tokens_spec, P("expert", None, None)),
        out_specs=(tokens_spec, P("expert", "dp", None)),
        check_vma=False,
    )
```

time: 148 us -> 89.8 us (0.61)
  Pallas kernels: 0 us -> 81.8 us
  waiting for transfers between devices: 65.7 us -> 0 us
  blocking collectives: 27.7 us -> 0 us
  matrix products: 17.4 us -> 0 us
  between operations: 14.1 us -> 0.64 us
  starting transfers between devices: 9.9 us -> 0 us
  other arithmetic: 9.85 us -> 0 us
  local copies, waits for them, and re-layouts: 2.47 us -> 7.02 us
    pallas_call x0 -> x1, Pallas kernels: none -> 81.8 us  [local(): pl.pallas_call(functools.partial(body, n_expert, n_dp, cap), out_shape=(j...]
    all_to_all x2 -> x0, waiting for transfers between devices: 45.5 us -> none  [the longest x1 23.2 us: local(): lax.all_to_all(send_x, 'expert', split_axis=0, concat_axis=0, tiled=True)]
    all_to_all x1 -> x0, blocking collectives: 27.7 us -> none  [send_back(): lax.all_to_all(returned, 'expert', split_axis=0, concat_axis=0, tiled=True)]
    reduce_scatter x1 -> x0, waiting for transfers between devices: 20.2 us -> none  [sum_weights(): lax.psum_scatter(weight_term(rows_in, grad_in, hidden, grad_pair, grad_sc...]
    dot_general x8 -> x0, matrix products: 17.4 us -> none  [the longest x1 3.69 us: weight_term(): lax.dot_general(rows_in, grad_pair, contract, preferred_element_type=jnp....]
    all_to_all x2 -> x0, starting transfers between devices: 9.86 us -> none  [the longest x1 6.35 us: local(): lax.all_to_all(send_x, 'expert', split_axis=0, concat_axis=0, tiled=True)]
    convert_element_type x2 -> x0, other arithmetic: 7.04 us -> none  [the longest x1 6.25 us: sum_weights(): weight_term(rows_in, grad_in, hidden, grad_pair, grad_scale)]
    unnamed x11 -> x4, local copies, waits for them, and re-layouts: 2.47 us -> 7.02 us
  transfers between devices with their start and end apart: 3 -> 0, of which waited for: 3 -> 0; matrix products, arithmetic and copies ran while one was open for 6% -> 0% of each run, Pallas kernels for 0% -> 0%
where the time goes in v1:
time: 89.8 us; the launch traced here: 89.4 us
  Pallas kernels  81.8 us (91%)
  local copies, waits for them, and re-layouts  7.02 us (8%)
    pallas_call x1, Pallas kernels, local(): pl.pallas_call(functools.partial(body, n_expert, n_dp, cap), out_shape=(j...  81.8 us
    unnamed x4, local copies, waits for them, and re-layouts  7.02 us

profile of v1, /device:TPU:0, one launch (start us, length us, event | category | flops | bytes accessed | tf_op | source)
XLA Modules:
  0.0 89.4 jit_solution(6148610464920265866)
XLA Ops:
  0.6 1.4 %copy.7.gate_ref = f32[128,1]{1,0:T(8,128)} copy(f32[128,1]{0,1:T(1,128)} %param.7) | data formatting | bytes 1024 | tf_op args[2]
  2.0 1.4 %copy.8.route_col_ref = s32[128,1]{1,0:T(8,128)} copy(s32[128,1]{0,1:T(1,128)} %param.8) | data formatting | bytes 1024 | tf_op args[3]
  3.4 81.8 %moe_backward.1 = (bf16[128,2048]{1,0:T(8,128)(2,1)}, f32[1,256,1152]{2,1,0:T(8,128)}) custom-call(bf16[128,2048]{1,0:T(8,128)(2,1)} %tokens_ref.1, bf16[128,2048]{1,0:T(8,128)(2,1)} %out_grad_ref.1, f32[128,1]{1,0:T(8,128)} %copy.7.gate_ref, s32[128,1]{1,0:T(8,128)} %copy.8.route_col_ref, s32[1,128]{1,0:T(1,128)} %bitcast.1, bf16[1,2048,1152]{2,1,0:T(8,128)(2,1)} %w_hbm.1), custom_call_target="tpu_custom_call" | custom-call | tf_op jit(solution)/shard_map/moe_backward/pallas_call | solution.py:350
  85.2 1.9 %copy.11 = bf16[128,2048]{1,0:T(8,128)(2,1)} copy(bf16[128,2048]{1,0:T(8,128)(2,1)} %get-tuple-element.4) | data formatting | bytes 1048576
  87.1 2.4 %copy.12 = f32[1,256,1152]{2,1,0:T(8,128)} copy(f32[1,256,1152]{2,1,0:T(8,128)} %get-tuple-element.5) | data formatting | bytes 2359296

commit v2 on v1

--- a/solution.py
+++ b/solution.py
@@ -10,6 +10,7 @@
 MESH = pl.DeviceIdType.MESH
 F32 = jnp.float32
 BF16 = jnp.bfloat16
+SUBS = 2
 
 
 def xor(value, step):
@@ -23,14 +24,15 @@
 
 
 def plan(n_expert, n_dp):
-    half = n_expert // 2
+    half, quarter = n_expert // 2, n_expert // 4
     near = list(range(1, half))
-    far = list(range(n_expert - 1, half - 1, -1))
+    across = list(range(n_expert - 1, half + quarter - 1, -1))
+    last = list(range(half + quarter - 1, half - 1, -1))
     chips = n_dp // 2
     side = math.isqrt(chips)
     while chips % side:
         side -= 1
-    return near, far, chips // side, side
+    return near, across, last, chips // side, side
 
 
 def body(
@@ -74,14 +76,16 @@
     c_s,
     c_r,
 ):
-    near, far, na, nb = plan(n_expert, n_dp)
+    near, across, last, na, nb = plan(n_expert, n_dp)
+    far = across + last
     me = lax.axis_index("expert")
     dp = lax.axis_index("dp")
     tok, width = tokens_ref.shape
     hid = w_ref.shape[1] // 3
     slots = n_expert * cap
-    half_rows = slots // 2
+    quarter_rows = slots // 4
     share = width // n_dp
+    sub = share // SUBS
     grad_scale = float(tok * n_dp) ** (-0.5)
     core = lax.rem(dp, 2)
     chip = lax.div(dp, 2)
@@ -168,10 +172,10 @@
     recv_g[rows_of(me)] = send_g[rows_of(me)]
     w_copy.wait()
 
-    mine = lax.div(me, n_expert // 2) if n_expert > 1 else 0
-
-    def forward(start):
-        rows = pl.ds(pl.multiple_of(start, cap), half_rows)
+    mine = lax.div(me, n_expert // 4)
+
+    def forward(start, size):
+        rows = pl.ds(pl.multiple_of(start, cap), size)
         x = recv_x[rows]
         pre_gate = jnp.dot(x, w_ref[:, :hid], preferred_element_type=F32)
         pre_up = jnp.dot(x, w_ref[:, hid : 2 * hid], preferred_element_type=F32)
@@ -183,8 +187,8 @@
         pair[rows, :hid] = grad_gate.astype(BF16)
         pair[rows, hid:] = (grad_hidden * active).astype(BF16)
 
-    def backward(start):
-        rows = pl.ds(pl.multiple_of(start, cap), half_rows)
+    def backward(start, size):
+        rows = pl.ds(pl.multiple_of(start, cap), size)
         tile = min(512, width)
 
         @pl.loop(0, width // tile)
@@ -197,23 +201,28 @@
                 preferred_element_type=F32,
             ).astype(BF16)
 
-    first_half = mine * half_rows
-    other_half = (1 - mine) * half_rows
+    near_half = (lax.div(mine, 2) * 2 * quarter_rows, 2 * quarter_rows)
+    across_quarter = (xor(mine, 3) * quarter_rows, quarter_rows)
+    last_quarter = (xor(mine, 2) * quarter_rows, quarter_rows)
     for k in near:
         x_copies[k].wait_recv()
         g_copies[k].wait_recv()
-    forward(first_half)
-    backward(first_half)
+    forward(*near_half)
+    backward(*near_half)
     for k in near:
         returns[k].start()
     arrived[rows_of(me)] = ret[rows_of(me)]
-    for k in far:
+    for k in across:
         x_copies[k].wait_recv()
         g_copies[k].wait_recv()
-    forward(other_half)
-    backward(other_half)
-    for k in far:
+    forward(*across_quarter)
+    backward(*across_quarter)
+    for k in last:
+        x_copies[k].wait_recv()
+        g_copies[k].wait_recv()
+    for k in across:
         returns[k].start()
+    forward(*last_quarter)
 
     def weight_rows(start, size):
         at = pl.ds(pl.multiple_of(start, size), size)
@@ -227,11 +236,12 @@
             * lax.dot_general(recv_g[:, at], hidden[...], contract, preferred_element_type=F32)
         ).astype(BF16)
 
-    def band(chip_at, core_at):
-        return pl.ds(pl.multiple_of((chip_at * 2 + core_at) * share, share), share)
-
-    items = [(s, t) for s in range(1, na) for t in list(range(1, nb)) + [0]]
-    items += [(0, t) for t in list(range(1, nb)) + [0]]
+    def band(chip_at, core_at, g):
+        return pl.ds(pl.multiple_of((chip_at * 2 + core_at) * share + g * sub, sub), sub)
+
+    bands = [(s, t) for s in range(1, na) for t in list(range(1, nb)) + [0]]
+    bands += [(0, t) for t in list(range(1, nb)) + [0]]
+    items = [(s, t, g) for s, t in bands for g in range(SUBS)]
 
     def item_chip(s, t):
         return chip_of(lax.rem(a + s, na), lax.rem(b + t, nb))
@@ -243,11 +253,11 @@
         def _(j):
             weight_rows(j * 256, 256)
 
-    def pair_copy(index, chip_at):
-        rows = band(chip_at, 1 - core)
+    def pair_copy(index, chip_at, g):
+        rows = band(chip_at, 1 - core, g)
         return pltpu.make_async_remote_copy(
             src_ref=part.at[rows],
-            dst_ref=recv_a.at[pl.ds(pl.multiple_of(chip_at * share, share), share)],
+            dst_ref=recv_a.at[pl.ds(pl.multiple_of(chip_at * share + g * sub, sub), sub)],
             send_sem=a_s.at[index],
             recv_sem=a_r.at[index],
             device_id={"dp": partner},
@@ -261,32 +271,36 @@
         return item_chip(s, t)
 
     a_copies = []
-    for index, (s, t) in enumerate(items):
+    for index, (s, t, g) in enumerate(items):
         chip_at = partner_chip(s, t)
-        if banded:
+        if banded and g == 0:
             weight_rows((chip_at * 2 + 1 - core) * share, share)
-        copy = pair_copy(index, chip_at)
+        copy = pair_copy(index, chip_at, g)
         copy.start()
         a_copies.append(copy)
 
-    def pair_sum(index, s, t):
+    backward(*last_quarter)
+    for k in last:
+        returns[k].start()
+
+    def pair_sum(index, s, t, g):
         chip_at = item_chip(s, t)
         a_copies[index].wait_recv()
         return (
-            part[band(chip_at, core)].astype(F32)
-            + recv_a[pl.ds(pl.multiple_of(chip_at * share, share), share)].astype(F32)
+            part[band(chip_at, core, g)].astype(F32)
+            + recv_a[pl.ds(pl.multiple_of(chip_at * share + g * sub, sub), sub)].astype(F32)
         )
 
     if banded:
-        for s, t in items:
+        for s, t in bands:
             weight_rows((item_chip(s, t) * 2 + core) * share, share)
 
     b_copies = {}
-    for index, (s, t) in enumerate(items):
+    for index, (s, t, g) in enumerate(items):
         if s == 0:
             continue
-        at = (s - 1) * nb + t
-        send_b[at] = pair_sum(index, s, t).astype(BF16)
+        at = ((s - 1) * nb + t) * SUBS + g
+        send_b[at] = pair_sum(index, s, t, g).astype(BF16)
         copy = pltpu.make_async_remote_copy(
             src_ref=send_b.at[at],
             dst_ref=recv_b.at[at],
@@ -296,32 +310,34 @@
             device_id_type=MESH,
         )
         copy.start()
-        b_copies[s, t] = copy
+        b_copies[s, t, g] = copy
     c_copies = {}
-    for index, (s, t) in enumerate(items):
+    for index, (s, t, g) in enumerate(items):
         if s > 0:
             continue
-        total = pair_sum(index, s, t)
+        total = pair_sum(index, s, t, g)
         for s_from in range(1, na):
-            b_copies[s_from, t].wait_recv()
-            total = total + recv_b[(s_from - 1) * nb + t].astype(F32)
+            b_copies[s_from, t, g].wait_recv()
+            total = total + recv_b[((s_from - 1) * nb + t) * SUBS + g].astype(F32)
         if t > 0:
-            send_c[t - 1] = total.astype(BF16)
+            at = (t - 1) * SUBS + g
+            send_c[at] = total.astype(BF16)
             copy = pltpu.make_async_remote_copy(
-                src_ref=send_c.at[t - 1],
-                dst_ref=recv_c.at[t - 1],
-                send_sem=c_s.at[t - 1],
-                recv_sem=c_r.at[t - 1],
+                src_ref=send_c.at[at],
+                dst_ref=recv_c.at[at],
+                send_sem=c_s.at[at],
+                recv_sem=c_r.at[at],
                 device_id={"dp": dp_of(a, lax.rem(b + t, nb))},
                 device_id_type=MESH,
             )
             copy.start()
-            c_copies[t] = copy
+            c_copies[t, g] = copy
         else:
-            w_grad_ref[0] = total
+            w_grad_ref[0, pl.ds(g * sub, sub)] = total
     for t in range(1, nb):
-        c_copies[t].wait_recv()
-        w_grad_ref[0] += recv_c[t - 1].astype(F32)
+        for g in range(SUBS):
+            c_copies[t, g].wait_recv()
+            w_grad_ref[0, pl.ds(g * sub, sub)] += recv_c[(t - 1) * SUBS + g].astype(F32)
 
     for k in near + far:
         returns[k].wait_recv()
@@ -342,9 +358,10 @@
     cap = max(16, 2 * tok // n_expert)
     slots = n_expert * cap
     share = width // n_dp
-    _, _, na, nb = plan(n_expert, n_dp)
+    _, _, _, na, nb = plan(n_expert, n_dp)
+    sub = share // SUBS
     chips = na * nb
-    n_b, n_c = max(1, (na - 1) * nb), max(1, nb - 1)
+    n_b, n_c = max(1, (na - 1) * nb) * SUBS, max(1, nb - 1) * SUBS
     dma = pltpu.SemaphoreType.DMA
     vmem = pl.BlockSpec(memory_space=pltpu.VMEM)
     return pl.pallas_call(
@@ -367,10 +384,10 @@
             pltpu.VMEM((slots, hid), BF16),
             pltpu.VMEM((width, full), BF16),
             pltpu.VMEM((chips * share, full), BF16),
-            pltpu.VMEM((n_b, share, full), BF16),
-            pltpu.VMEM((n_b, share, full), BF16),
-            pltpu.VMEM((n_c, share, full), BF16),
-            pltpu.VMEM((n_c, share, full), BF16),
+            pltpu.VMEM((n_b, sub, full), BF16),
+            pltpu.VMEM((n_b, sub, full), BF16),
+            pltpu.VMEM((n_c, sub, full), BF16),
+            pltpu.VMEM((n_c, sub, full), BF16),
             dma,
             dma((n_expert,)),
             dma((n_expert,)),
@@ -378,8 +395,8 @@
             dma((n_expert,)),
             dma((n_expert,)),
             dma((n_expert,)),
-            dma((chips,)),
-            dma((chips,)),
+            dma((chips * SUBS,)),
+            dma((chips * SUBS,)),
             dma((n_b,)),
             dma((n_b,)),
             dma((n_c,)),

time: 89.8 us -> 90.4 us (level)
  no operation moved by 1% of the time
where the time goes in v2:
time: 90.4 us; the launch traced here: 90.1 us
  Pallas kernels  82.5 us (91%)
  local copies, waits for them, and re-layouts  7.02 us (8%)
    pallas_call x1, Pallas kernels, local(): pl.pallas_call(functools.partial(body, n_expert, n_dp, cap), out_shape=(j...  82.5 us
    unnamed x4, local copies, waits for them, and re-layouts  7.02 us

profile of v2, /device:TPU:0, one launch (start us, length us, event | category | flops | bytes accessed | tf_op | source)
XLA Modules:
  0.0 90.1 jit_solution(7752397078696389695)
XLA Ops:
  0.6 1.4 %copy.7.gate_ref = f32[128,1]{1,0:T(8,128)} copy(f32[128,1]{0,1:T(1,128)} %param.7) | data formatting | bytes 1024 | tf_op args[2]
  2.0 1.4 %copy.8.route_col_ref = s32[128,1]{1,0:T(8,128)} copy(s32[128,1]{0,1:T(1,128)} %param.8) | data formatting | bytes 1024 | tf_op args[3]
  3.4 82.5 %moe_backward.1 = (bf16[128,2048]{1,0:T(8,128)(2,1)}, f32[1,256,1152]{2,1,0:T(8,128)}) custom-call(bf16[128,2048]{1,0:T(8,128)(2,1)} %tokens_ref.1, bf16[128,2048]{1,0:T(8,128)(2,1)} %out_grad_ref.1, f32[128,1]{1,0:T(8,128)} %copy.7.gate_ref, s32[128,1]{1,0:T(8,128)} %copy.8.route_col_ref, s32[1,128]{1,0:T(1,128)} %bitcast.1, bf16[1,2048,1152]{2,1,0:T(8,128)(2,1)} %w_hbm.1), custom_call_target="tpu_custom_call" | custom-call | tf_op jit(solution)/shard_map/moe_backward/pallas_call | solution.py:367
  85.9 1.9 %copy.11 = bf16[128,2048]{1,0:T(8,128)(2,1)} copy(bf16[128,2048]{1,0:T(8,128)(2,1)} %get-tuple-element.4) | data formatting | bytes 1048576
  87.8 2.4 %copy.12 = f32[1,256,1152]{2,1,0:T(8,128)} copy(f32[1,256,1152]{2,1,0:T(8,128)} %get-tuple-element.5) | data formatting | bytes 2359296

commit v3 on v2

--- a/solution.py
+++ b/solution.py
@@ -11,6 +11,7 @@
 F32 = jnp.float32
 BF16 = jnp.bfloat16
 SUBS = 2
+PIECES = 4
 
 
 def xor(value, step):
@@ -42,8 +43,7 @@
     tokens_ref,
     out_grad_ref,
     gate_ref,
-    route_col_ref,
-    route_row_ref,
+    route_ref,
     w_hbm,
     in_grad_ref,
     w_grad_ref,
@@ -127,22 +127,26 @@
         )
         greeted += 1
 
-    route_row = route_row_ref[...]
-    route_col = route_col_ref[...]
     row_i = lax.broadcasted_iota(jnp.int32, (tok, tok), 0)
     col_i = lax.broadcasted_iota(jnp.int32, (tok, tok), 1)
+
+    def column(row):
+        return jnp.sum(jnp.where(row_i == col_i, row, 0.0), axis=1, keepdims=True)
+
+    route_row = route_ref[...].astype(F32)
+    route_col = column(route_row)
     same = route_col == route_row
     pos_row = jnp.sum(jnp.where(same & (row_i < col_i), 1.0, 0.0), axis=0, keepdims=True)
     pos_col = jnp.sum(jnp.where(same & (col_i < row_i), 1.0, 0.0), axis=1, keepdims=True)
-    slot_row = route_row.astype(F32) * cap + pos_row
-    slot_col = route_col.astype(F32) * cap + pos_col
+    slot_row = route_row * cap + pos_row
+    slot_col = route_col * cap + pos_col
     slot_at = lax.broadcasted_iota(jnp.int32, (slots, tok), 0).astype(F32)
     table = jnp.where(slot_at == slot_row, 1.0, 0.0).astype(BF16)
     slot_of = lax.broadcasted_iota(jnp.int32, (tok, slots), 1).astype(F32)
     table_t = jnp.where(slot_of == slot_col, 1.0, 0.0).astype(BF16)
 
     send_x[...] = jnp.dot(table, tokens_ref[...], preferred_element_type=F32).astype(BF16)
-    scaled = (gate_ref[...] * out_grad_ref[...].astype(F32)).astype(BF16)
+    scaled = (column(gate_ref[...]) * out_grad_ref[...].astype(F32)).astype(BF16)
     send_g[...] = jnp.dot(table, scaled, preferred_element_type=F32).astype(BF16)
 
     def rows_of(index):
@@ -364,13 +368,13 @@
     n_b, n_c = max(1, (na - 1) * nb) * SUBS, max(1, nb - 1) * SUBS
     dma = pltpu.SemaphoreType.DMA
     vmem = pl.BlockSpec(memory_space=pltpu.VMEM)
-    return pl.pallas_call(
+    early = pl.pallas_call(
         functools.partial(body, n_expert, n_dp, cap),
         out_shape=(
             jax.ShapeDtypeStruct((tok, width), BF16),
             jax.ShapeDtypeStruct((1, share, full), F32),
         ),
-        in_specs=[vmem] * 5 + [pl.BlockSpec(memory_space=pl.ANY)],
+        in_specs=[vmem] * 4 + [pl.BlockSpec(memory_space=pl.ANY)],
         out_specs=(vmem, vmem),
         scratch_shapes=[
             pltpu.VMEM((width, full), BF16),
@@ -406,7 +410,48 @@
             collective_id=0, has_side_effects=True, vmem_limit_bytes=60 * 1024 * 1024
         ),
         name="moe_backward",
-    )(tokens, out_grad, gate_prob, routing, routing.reshape(1, tok), expert_weights)
+    )(tokens, out_grad, gate_prob.reshape(1, tok), routing.reshape(1, tok), expert_weights)
+    return pl.pallas_call(
+        write_out,
+        out_shape=(
+            jax.ShapeDtypeStruct((tok, width), BF16),
+            jax.ShapeDtypeStruct((1, share, full), F32),
+        ),
+        in_specs=[pl.BlockSpec(memory_space=pl.ANY)] * 2,
+        out_specs=(pl.BlockSpec(memory_space=pl.ANY),) * 2,
+        scratch_shapes=[
+            pltpu.VMEM((tok, width), BF16),
+            pltpu.VMEM((1, share, full), F32),
+            dma((2 * PIECES,)),
+            dma((2 * PIECES,)),
+        ],
+        name="write_out",
+    )(*early)
+
+
+def write_out(in_grad_ref, w_grad_ref, in_grad_out, w_grad_out, x_held, w_held, in_s, out_s):
+    moves = []
+    for p in range(PIECES):
+        for src, mid, dst in (
+            (in_grad_ref, x_held, in_grad_out),
+            (w_grad_ref.at[0], w_held.at[0], w_grad_out.at[0]),
+        ):
+            rows = src.shape[0] // PIECES
+            at = pl.ds(p * rows, rows)
+            n = len(moves)
+            moves.append(
+                (
+                    pltpu.make_async_copy(src.at[at], mid.at[at], in_s.at[n]),
+                    pltpu.make_async_copy(mid.at[at], dst.at[at], out_s.at[n]),
+                )
+            )
+    for take, _ in moves:
+        take.start()
+    for take, put in moves:
+        take.wait()
+        put.start()
+    for _, put in moves:
+        put.wait()
 
 
 def solution(mesh):

time: 90.4 us -> 85.6 us (0.947)
  local copies, waits for them, and re-layouts: 7.02 us -> 0 us
  Pallas kernels: 82.5 us -> 84.8 us
    unnamed x4 -> x0, local copies, waits for them, and re-layouts: 7.02 us -> none
    pallas_call x0 -> x1, Pallas kernels: none -> 2.32 us  [local(): pl.pallas_call(write_out, out_shape=(jax.ShapeDtypeStruct((tok, width), B...]
where the time goes in v3:
time: 85.6 us; the launch traced here: 85.4 us
  Pallas kernels  84.8 us (99%)
    pallas_call x1, Pallas kernels, local(): pl.pallas_call(functools.partial(body, n_expert, n_dp, cap), out_shape=(j...  82.5 us
    pallas_call x1, Pallas kernels, local(): pl.pallas_call(write_out, out_shape=(jax.ShapeDtypeStruct((tok, width), B...  2.32 us

profile of v3, /device:TPU:0, one launch (start us, length us, event | category | flops | bytes accessed | tf_op | source)
XLA Modules:
  0.0 85.4 jit_solution(8406087684264835199)
XLA Ops:
  0.6 82.5 %moe_backward.1 = (bf16[128,2048]{1,0:T(8,128)(2,1)}, f32[1,256,1152]{2,1,0:T(8,128)}) custom-call(bf16[128,2048]{1,0:T(8,128)(2,1)} %tokens_ref.1, bf16[128,2048]{1,0:T(8,128)(2,1)} %out_grad_ref.1, f32[1,128]{1,0:T(1,128)} %bitcast.2, s32[1,128]{1,0:T(1,128)} %bitcast.3, bf16[1,2048,1152]{2,1,0:T(8,128)(2,1)} %w_hbm.1), custom_call_target="tpu_custom_call" | custom-call | tf_op jit(solution)/shard_map/moe_backward/pallas_call | solution.py:371
  83.1 2.3 %write_out.1 = (bf16[128,2048]{1,0:T(8,128)(2,1)}, f32[1,256,1152]{2,1,0:T(8,128)}) custom-call(bf16[128,2048]{1,0:T(8,128)(2,1)} %get-tuple-element.4.in_grad_ref, f32[1,256,1152]{2,1,0:T(8,128)} %get-tuple-element.5.w_grad_ref), custom_call_target="tpu_custom_call" | custom-call | tf_op jit(solution)/shard_map/write_out/pallas_call | solution.py:414
